TPU v7x, 256 devices: a whole 4x4x8 slice. The times are simulated.
256 devices in a mesh: dp: 32 (over y, z_lo, x), tensor: 8 (over z_hi, core).
Axes of the slice: x: 4, y: 4, z: 8 (z_hi: 4, z_lo: 2; z = z_hi * 2 + z_lo), core: 2. Of those that a mesh axis runs over, the one named last changes fastest.
Arguments:
- hidden: bfloat16 [32768, 7168], P('dp', 'tensor'), parts along dimension 0, may hold values from -6 to 6
- w_dq: bfloat16 [7168, 1536], P('tensor'), may hold values from -0.0625 to 0.0625
- w_dkv: bfloat16 [7168, 576], P('tensor'), may hold values from -0.0625 to 0.0625
- q_gain: float32 [1536], replicated, may hold values from 0.1 to 1.9
- kv_gain: float32 [512], replicated, may hold values from 0.1 to 1.9
- w_uq: bfloat16 [1536, 12288], P(None, 'tensor'), may hold values from -0.15625 to 0.15625
- w_ukv: bfloat16 [512, 16384], P(None, 'tensor'), may hold values from -0.25 to 0.25
Outputs:
- queries: bfloat16 [32768, 12288], P('dp', 'tensor'), parts along dimension 0
- keys_values: bfloat16 [32768, 16384], P('dp', 'tensor'), parts along dimension 0
- rotary_key: bfloat16 [32768, 64], P(('dp', 'tensor')), parts along dimension 0
There are 32 independent parts, one for each index of `dp`. A program takes and returns all parts, laid end to end along the dimension named above; an argument that names none is the same for every part. Nothing has to cross between parts.
All inputs are finite; a program needn't handle non-finite values.
Results may differ from a plain program's by a relative error of at most 0.0049.
Values may be sent and summed in bfloat16 or wider, within the bound.
No kernel may reach another device: no remote copies, remote signals or barrier semaphores. Data moves between devices by JAX's collectives and lax.ppermute only.
A program may use at most 128 MiB of HBM per device.

v0:
```python
import jax
import jax.numpy as jnp
from jax import lax
from jax.sharding import PartitionSpec as P

NOPE = 128
ROPE = 64


def rotate(values, angle):
    half = values.shape[-1] // 2
    first = values[..., :half]
    second = values[..., half:]
    cosine = jnp.cos(angle)
    sine = jnp.sin(angle)
    return jnp.concatenate(
        [first * cosine - second * sine, second * cosine + first * sine], axis=-1
    )


def angles(first_row, count, half):
    positions = (first_row + lax.iota(jnp.int32, count)).astype(jnp.float32)
    freqs = 50000.0 ** (-jnp.arange(half, dtype=jnp.float32) / half)
    return positions[:, None] * freqs[None, :]


def normalize(block, gain):
    scale = lax.rsqrt(jnp.mean(block * block, axis=1, keepdims=True) + 1e-06)
    return (block * scale * gain[None, :]).astype(jnp.bfloat16)


def shards(hidden, w_dq, w_dkv, q_gain, kv_gain, w_uq, w_ukv):
    q_width = w_dq.shape[1]
    kv_width = kv_gain.shape[0]
    rope_width = w_dkv.shape[1] - kv_width
    head_width = NOPE + ROPE
    local_heads = w_uq.shape[1] // head_width
    total_rows = hidden.shape[0]
    share = total_rows // lax.axis_size("tensor")
    own_start = lax.axis_index("tensor") * share
    down = lax.psum_scatter(
        jnp.concatenate(
            [
                jnp.dot(hidden, w_dq, preferred_element_type=jnp.float32),
                jnp.dot(hidden, w_dkv, preferred_element_type=jnp.float32),
            ],
            axis=1,
        ),
        "tensor",
        scatter_dimension=0,
        tiled=True,
    )
    latent = jnp.concatenate(
        [
            normalize(down[:, :q_width], q_gain),
            normalize(down[:, q_width : q_width + kv_width], kv_gain),
        ],
        axis=1,
    )
    piece = lax.all_gather(latent, "tensor", axis=0, tiled=True)
    count = piece.shape[0]
    query_full = jnp.dot(piece[:, :q_width], w_uq, preferred_element_type=jnp.float32)
    query_full = query_full.reshape(count, local_heads, head_width)
    angle = angles(jnp.int32(0), count, ROPE // 2)
    turned = rotate(query_full[:, :, NOPE:], angle[:, None, :])
    query_out = jnp.concatenate([query_full[:, :, :NOPE], turned], axis=2)
    query_out = query_out.reshape(count, local_heads * head_width).astype(jnp.bfloat16)
    kv_out = jnp.dot(piece[:, q_width:], w_ukv, preferred_element_type=jnp.float32).astype(
        jnp.bfloat16
    )
    both = jnp.concatenate([query_out, kv_out], axis=1)
    mine = down[:, q_width + kv_width :]
    rotary_key = rotate(mine, angles(own_start, share, rope_width // 2)).astype(jnp.bfloat16)
    query_cols = local_heads * head_width
    return (both[:, :query_cols], both[:, query_cols:], rotary_key)


def solution(mesh):
    in_specs = (
        P("dp", "tensor"),
        P("tensor", None),
        P("tensor", None),
        P(),
        P(),
        P(None, "tensor"),
        P(None, "tensor"),
    )
    out_specs = (P("dp", "tensor"), P("dp", "tensor"), P(("dp", "tensor"), None))
    return jax.shard_map(shards, mesh=mesh, in_specs=in_specs, out_specs=out_specs, check_vma=False)
```

profile of v0, /device:TPU:1, one launch (start us, length us, event | category | flops | bytes accessed | tf_op | source)
XLA Modules:
  0.0 218.4 jit_solution(12857306435849263300)
XLA Ops:
  7.2 0.0 copy-start
  7.2 0.0 reduce-scatter.2.cloned.1.call-start
  7.2 1.7 copy-done
  8.9 0.0 copy-start.3
  9.0 0.0 copy-start.4
  9.0 5.2 %fusion.11 = f32[1024,1536]{0,1:T(8,128)S(1)} fusion(bf16[1024,896]{1,0:T(8,128)(2,1)} %param.7, bf16[896,1536]{1,0:T(8,128)(2,1)S(1)} %copy-done), kind=kOutput, calls=%fused_computation.32 | convolution fusion | flops 2818572288 | bytes 10878976 | tf_op jit(solution)/shard_map/dot_general | solution.py:44
  14.2 0.0 copy-done.3
  14.2 0.0 copy-done.4
  14.2 2.8 %fusion.12 = f32[1024,576]{0,1:T(8,128)} fusion(bf16[1024,896]{1,0:T(8,128)(2,1)S(1)} %copy-done.3, bf16[896,576]{0,1:T(8,128)(2,1)S(1)} %copy-done.4), kind=kOutput, calls=%fused_computation.33 | convolution fusion | flops 1056964608 | bytes 5226496 | tf_op jit(solution)/shard_map/dot_general | solution.py:45
  17.0 6.4 %pad_maximum_fusion = f32[1024,2112]{0,1:T(8,128)} fusion(f32[1024,576]{0,1:T(8,128)} %fusion.12, f32[1024,1536]{0,1:T(8,128)S(1)} %fusion.11), kind=kLoop, calls=%fused_computation | loop fusion | flops 2162688 | bytes 17301504 | tf_op jit(solution)/shard_map/concatenate | solution.py:42
  23.4 0.0 copy-start.1
  23.4 0.0 reduce-scatter.2.cloned.1.call-update
  23.4 0.2 all-gather.2.cloned.1.call-start
  23.7 101.5 %reduce-scatter.2.cloned.1.call-done = f32[128,2112]{0,1:T(8,128)} async-done(((f32[1024,2112]{0,1:T(8,128)}), f32[128,2112]{0,1:T(8,128)}) %reduce-scatter.2.cloned.1.call-update) | async-done | bytes 1081360 | tf_op jit(solution)/shard_map/reduce_scatter | solution.py:41
  125.2 1.3 multiply_reduce_fusion
  126.5 1.0 multiply_reduce_fusion.1
  127.6 0.0 copy-done.1
  127.6 1.4 multiply_convert_fusion
  129.0 0.0 copy-done.2
  129.0 1.1 multiply_convert_fusion.1
  130.1 0.8 pad_maximum_fusion.2
  130.9 0.0 all-gather.2.cloned.1.call-update
  131.0 0.5 multiply_cosine_fusion
  131.5 0.9 fusion.8
  132.4 0.6 pad_maximum_fusion.3
  133.0 57.0 %all-gather.2.cloned.1.call-done = bf16[1024,2048]{0,1:T(8,128)(2,1)} async-done(((bf16[128,2048]{0,1:T(8,128)(2,1)}), bf16[1024,2048]{0,1:T(8,128)(2,1)}) %all-gather.2.cloned.1.call-update) | async-done | bytes 4194320 | tf_op jit(solution)/shard_map/all_gather | solution.py:60
  190.0 8.1 %fusion = f32[1024,1536]{0,1:T(8,128)S(1)} fusion(bf16[1536,1536]{1,0:T(8,128)(2,1)} %param.12, bf16[1024,2048]{0,1:T(8,128)(2,1)} %all-gather.2.cloned.1.call-done), kind=kOutput, calls=%fused_computation.3 | convolution fusion | flops 4831838208 | bytes 14155776 | tf_op jit(solution)/shard_map/dot_general | solution.py:62
  198.1 0.3 slice.69
  198.5 0.3 subtract_convert_fusion
  198.8 1.9 pad_maximum_fusion.1
  200.7 4.6 %copy.18 = bf16[1024,1536]{1,0:T(8,128)(2,1)} copy(bf16[1024,1536]{0,1:T(8,128)(2,1)} %bitcast.8) | data formatting | bytes 6291456
  205.3 6.3 %convolution_convert_fusion = bf16[1024,2048]{1,0:T(8,128)(2,1)} fusion(bf16[512,2048]{1,0:T(8,128)(2,1)} %param.13, bf16[1024,2048]{0,1:T(8,128)(2,1)} %all-gather.2.cloned.1.call-done), kind=kOutput, calls=%fused_computation.2 | convolution fusion | flops 2149580800 | bytes 7340032 | tf_op jit(solution)/shard_map/dot_general | solution.py:68
  (6 shorter events, 0.0 us)
Async XLA Ops:
  7.2 1.8 copy-start
  7.2 118.0 %reduce-scatter.2.cloned.1.call-start = ((), (), s32[]{:S(2)}) async-start(), calls=%async_computation.1 | async-start | bytes 9732096 | tf_op jit(solution)/shard_map/reduce_scatter | solution.py:41
  8.9 5.2 %copy-start.3 = (bf16[1024,896]{1,0:T(8,128)(2,1)S(1)}, bf16[1024,896]{1,0:T(8,128)(2,1)}, u32[]{:S(2)}) copy-start(bf16[1024,896]{1,0:T(8,128)(2,1)} %param.7) | copy-start | bytes 5505028
  9.0 5.2 %copy-start.4 = (bf16[896,576]{0,1:T(8,128)(2,1)S(1)}, bf16[896,576]{0,1:T(8,128)(2,1)}, u32[]{:S(2)}) copy-start(bf16[896,576]{0,1:T(8,128)(2,1)} %param.9) | copy-start | bytes 3096580
  23.4 104.2 %copy-start.1 = (f32[1536]{0:T(1024)S(1)}, f32[1536]{0:T(1024)}, u32[]{:S(2)}) copy-start(f32[1536]{0:T(1024)} %param.10) | copy-start | bytes 18436
  23.4 105.6 %copy-start.2 = (f32[512]{0:T(512)S(1)}, f32[512]{0:T(512)}, u32[]{:S(2)}) copy-start(f32[512]{0:T(512)} %param.11) | copy-start | bytes 6148
  23.4 166.5 %all-gather.2.cloned.1.call-start = ((), (), s32[]{:S(2)}) async-start(), calls=%async_computation.2 | async-start | bytes 4718592 | tf_op jit(solution)/shard_map/all_gather | solution.py:60
Sparse Core Ops, SparseCore 0:
  23.6 101.5 reduce-scatter.1
  131.0 58.8 all-gather.1
where the time goes:
time: 219 us; the launch traced here: 218 us
  waiting for transfers between devices  158 us (72%)
  matrix products  22.5 us (10%)
  other arithmetic  16.4 us (7%)
  between operations  14.1 us (6%)
  local copies, waits for them, and re-layouts  6.69 us (3%)
    reduce_scatter x1, waiting for transfers between devices, shards(): lax.psum_scatter(jnp.concatenate([jnp.dot(hidden, w_dq, preferred_element...  101 us
    all_gather x1, waiting for transfers between devices, shards(): piece = lax.all_gather(latent, 'tensor', axis=0, tiled=True)  57 us
    dot_general x1, matrix products, shards(): jnp.dot(piece[:, :q_width], w_uq, preferred_element_type=jnp.float32)  8.14 us
    concatenate x1, other arithmetic, shards(): jnp.concatenate([jnp.dot(hidden, w_dq, preferred_element_type=jnp.float32...  6.4 us
    unnamed x11, local copies, waits for them, and re-layouts  6.37 us
    dot_general x1, matrix products, shards(): jnp.dot(piece[:, q_width:], w_ukv, preferred_element_type=jnp.float32)  6.32 us
    dot_general x1, matrix products, shards(): jnp.dot(hidden, w_dq, preferred_element_type=jnp.float32)  5.2 us
  transfers between devices with their start and end apart: 2, of which 2 were waited for; matrix products, arithmetic and copies ran while one was open for 1% of the time, Pallas kernels for 0%

commit v1 on v0

--- a/solution.py
+++ b/solution.py
@@ -57,7 +57,9 @@
         ],
         axis=1,
     )
-    piece = lax.all_gather(latent, "tensor", axis=0, tiled=True)
+    piece = jnp.concatenate(
+        lax.all_to_all(jnp.stack([latent] * lax.axis_size("tensor")), "tensor", 0, 0), axis=0
+    )
     count = piece.shape[0]
     query_full = jnp.dot(piece[:, :q_width], w_uq, preferred_element_type=jnp.float32)
     query_full = query_full.reshape(count, local_heads, head_width)

time: 219 us -> 266 us (1.21)
  waiting for transfers between devices: 158 us -> 193 us
  starting transfers between devices: 0.26 us -> 9.23 us
  local copies, waits for them, and re-layouts: 6.69 us -> 10.5 us
    all_to_all x0 -> x1, waiting for transfers between devices: none -> 91.3 us  [shards(): lax.all_to_all(jnp.stack([latent] * lax.axis_size('tensor')), 'tensor', 0...]
    all_gather x1 -> x0, waiting for transfers between devices: 57 us -> none  [shards(): piece = lax.all_gather(latent, 'tensor', axis=0, tiled=True)]
    all_to_all x0 -> x1, starting transfers between devices: none -> 9.19 us  [shards(): lax.all_to_all(jnp.stack([latent] * lax.axis_size('tensor')), 'tensor', 0...]
where the time goes in v1:
time: 266 us
  waiting for transfers between devices  193 us (73%)
  matrix products  22.4 us (8%)
  other arithmetic  16.3 us (6%)
  between operations  14.1 us (5%)
  local copies, waits for them, and re-layouts  10.5 us (4%)
  starting transfers between devices  9.23 us (3%)
    reduce_scatter x1, waiting for transfers between devices, shards(): lax.psum_scatter(jnp.concatenate([jnp.dot(hidden, w_dq, preferred_element...  102 us
    all_to_all x1, waiting for transfers between devices, shards(): lax.all_to_all(jnp.stack([latent] * lax.axis_size('tensor')), 'tensor', 0...  91.3 us
    all_to_all x1, starting transfers between devices, shards(): lax.all_to_all(jnp.stack([latent] * lax.axis_size('tensor')), 'tensor', 0...  9.19 us
    dot_general x1, matrix products, shards(): jnp.dot(piece[:, :q_width], w_uq, preferred_element_type=jnp.float32)  8.12 us
    concatenate x1, other arithmetic, shards(): jnp.concatenate([jnp.dot(hidden, w_dq, preferred_element_type=jnp.float32...  6.39 us
    unnamed x11, local copies, waits for them, and re-layouts  6.37 us
    dot_general x1, matrix products, shards(): jnp.dot(piece[:, q_width:], w_ukv, preferred_element_type=jnp.float32)  6.28 us
  transfers between devices with their start and end apart: 2, of which 2 were waited for; matrix products, arithmetic and copies ran while one was open for 1% of the time, Pallas kernels for 0%

profile of v1, /device:TPU:1, one launch (start us, length us, event | category | flops | bytes accessed | tf_op | source)
XLA Modules:
  0.0 265.7 jit_solution(4853611331293507995)
XLA Ops:
  7.2 0.0 copy-start
  7.2 0.0 reduce-scatter.2.cloned.1.call-start
  7.2 1.7 copy-done
  8.9 0.0 copy-start.3
  9.0 0.0 copy-start.4
  9.0 5.2 %fusion.11 = f32[1024,1536]{0,1:T(8,128)S(1)} fusion(bf16[1024,896]{1,0:T(8,128)(2,1)} %param.7, bf16[896,1536]{1,0:T(8,128)(2,1)S(1)} %copy-done), kind=kOutput, calls=%fused_computation.32 | convolution fusion | flops 2818572288 | bytes 10878976 | tf_op jit(solution)/shard_map/dot_general | solution.py:44
  14.2 0.0 copy-done.3
  14.2 0.0 copy-done.4
  14.2 2.8 %fusion.12 = f32[1024,576]{0,1:T(8,128)} fusion(bf16[1024,896]{1,0:T(8,128)(2,1)S(1)} %copy-done.3, bf16[896,576]{0,1:T(8,128)(2,1)S(1)} %copy-done.4), kind=kOutput, calls=%fused_computation.33 | convolution fusion | flops 1056964608 | bytes 5226496 | tf_op jit(solution)/shard_map/dot_general | solution.py:45
  17.0 6.4 %pad_maximum_fusion = f32[1024,2112]{0,1:T(8,128)} fusion(f32[1024,576]{0,1:T(8,128)} %fusion.12, f32[1024,1536]{0,1:T(8,128)S(1)} %fusion.11), kind=kLoop, calls=%fused_computation | loop fusion | flops 2162688 | bytes 17301504 | tf_op jit(solution)/shard_map/concatenate | solution.py:42
  23.4 0.0 reduce-scatter.2.cloned.1.call-update
  23.4 101.7 %reduce-scatter.2.cloned.1.call-done = f32[128,2112]{0,1:T(8,128)} async-done(((f32[1024,2112]{0,1:T(8,128)}), f32[128,2112]{0,1:T(8,128)}) %reduce-scatter.2.cloned.1.call-update) | async-done | bytes 1081360 | tf_op jit(solution)/shard_map/reduce_scatter | solution.py:41
  125.1 1.3 multiply_reduce_fusion
  126.5 1.0 multiply_reduce_fusion.1
  127.5 0.0 copy-done.1
  127.6 1.4 multiply_convert_fusion
  129.0 0.0 copy-done.2
  129.0 1.1 multiply_convert_fusion.1
  130.1 0.8 pad_maximum_fusion.2
  130.9 1.2 copy.17
  132.1 2.6 stack.2
  134.7 9.2 %all-to-all-start = ((bf16[8,128,2048]{2,1,0:T(8,128)(2,1)}), bf16[8,128,2048]{2,1,0:T(8,128)(2,1)}, u32[]{:S(2)}, u32[]{:S(2)}) async-start(bf16[8,128,2048]{2,1,0:T(8,128)(2,1)} %stack.2), calls=%async_computation.1 | async-start | bytes 8388608 | tf_op jit(solution)/shard_map/all_to_all | solution.py:61
  143.9 0.5 multiply_cosine_fusion
  144.5 0.9 fusion.8
  145.4 0.6 pad_maximum_fusion.3
  146.0 91.3 %all-to-all-done = bf16[8,128,2048]{2,1,0:T(8,128)(2,1)} async-done(((bf16[8,128,2048]{2,1,0:T(8,128)(2,1)}), bf16[8,128,2048]{2,1,0:T(8,128)(2,1)}, u32[]{:S(2)}, u32[]{:S(2)}) %all-to-all-start) | async-done | bytes 4194336 | tf_op jit(solution)/shard_map/all_to_all | solution.py:61
  237.3 8.1 %fusion = f32[1024,1536]{0,1:T(8,128)S(1)} fusion(bf16[1536,1536]{1,0:T(8,128)(2,1)} %param.12, bf16[1024,2048]{1,0:T(8,128)(2,1)} %bitcast), kind=kOutput, calls=%fused_computation.3 | convolution fusion | flops 4831838208 | bytes 14155776 | tf_op jit(solution)/shard_map/dot_general | solution.py:64
  245.4 0.3 slice.69
  245.7 0.3 subtract_convert_fusion
  246.1 1.9 pad_maximum_fusion.1
  247.9 4.6 %copy.19 = bf16[1024,1536]{1,0:T(8,128)(2,1)} copy(bf16[1024,1536]{0,1:T(8,128)(2,1)} %bitcast.9) | data formatting | bytes 6291456
  252.6 6.3 %convolution_convert_fusion = bf16[1024,2048]{1,0:T(8,128)(2,1)} fusion(bf16[512,2048]{1,0:T(8,128)(2,1)} %param.13, bf16[1024,2048]{1,0:T(8,128)(2,1)} %bitcast), kind=kOutput, calls=%fused_computation.2 | convolution fusion | flops 2149580800 | bytes 7340032 | tf_op jit(solution)/shard_map/dot_general | solution.py:70
  (7 shorter events, 0.0 us)
Async XLA Ops:
  7.2 1.8 copy-start
  7.2 118.0 %reduce-scatter.2.cloned.1.call-start = ((), (), s32[]{:S(2)}) async-start(), calls=%async_computation.2 | async-start | bytes 9732096 | tf_op jit(solution)/shard_map/reduce_scatter | solution.py:41
  8.9 5.2 %copy-start.3 = (bf16[1024,896]{1,0:T(8,128)(2,1)S(1)}, bf16[1024,896]{1,0:T(8,128)(2,1)}, u32[]{:S(2)}) copy-start(bf16[1024,896]{1,0:T(8,128)(2,1)} %param.7) | copy-start | bytes 5505028
  9.0 5.2 %copy-start.4 = (bf16[896,576]{0,1:T(8,128)(2,1)S(1)}, bf16[896,576]{0,1:T(8,128)(2,1)}, u32[]{:S(2)}) copy-start(bf16[896,576]{0,1:T(8,128)(2,1)} %param.9) | copy-start | bytes 3096580
  23.4 104.2 %copy-start.1 = (f32[1536]{0:T(1024)S(1)}, f32[1536]{0:T(1024)}, u32[]{:S(2)}) copy-start(f32[1536]{0:T(1024)} %param.10) | copy-start | bytes 18436
  23.4 105.6 %copy-start.2 = (f32[512]{0:T(512)S(1)}, f32[512]{0:T(512)}, u32[]{:S(2)}) copy-start(f32[512]{0:T(512)} %param.11) | copy-start | bytes 6148
  134.7 102.6 %all-to-all-start = ((bf16[8,128,2048]{2,1,0:T(8,128)(2,1)}), bf16[8,128,2048]{2,1,0:T(8,128)(2,1)}, u32[]{:S(2)}, u32[]{:S(2)}) async-start(bf16[8,128,2048]{2,1,0:T(8,128)(2,1)} %stack.2), calls=%async_computation.1 | async-start | bytes 8388608 | tf_op jit(solution)/shard_map/all_to_all | solution.py:61
Sparse Core Ops, SparseCore 0:
  23.5 101.5 reduce-scatter.1
